TPU v7x, 32 devices: a 4x4x1 block of a 4x4x8 slice. The times are simulated.
32 devices in a mesh: dp: 1 (over z), yax: 4 (over y), xax: 8 (over x, core).
Axes of the slice: x: 4, y: 4, z: 1, core: 2. Of those that a mesh axis runs over, the one named last changes fastest.
The devices are a block of a 4x4x8 slice.
Arguments:
- hidden: bfloat16 [1024, 1024], P('dp', 'xax')
- cache_len: int32 [1024], P('dp')
- k_cache: bfloat16 [1024, 4096, 64], P(('dp', 'yax', 'xax'))
- v_cache: bfloat16 [1024, 4096, 64], P(('dp', 'yax', 'xax'))
- g_attn: float32 [1024], P('xax')
- w_query: bfloat16 [1024, 1024], P('xax', 'yax')
- w_key: bfloat16 [1024, 64], P('xax')
- w_value: bfloat16 [1024, 64], P('xax')
- w_gate: bfloat16 [1024, 4096], P('xax', 'yax')
- w_up: bfloat16 [1024, 4096], P('xax', 'yax')
- w_out: bfloat16 [1024, 1024], P('yax', 'xax')
- w_down: bfloat16 [4096, 1024], P('yax', 'xax')
- g_final: float32 [1024], P('xax')
- embedding: bfloat16 [50304, 1024], P('yax', 'xax')
Outputs:
- output 1: bfloat16 [1024, 64], P(('dp', 'yax', 'xax'))
- output 2: bfloat16 [1024, 64], P(('dp', 'yax', 'xax'))
- output 3: float32 [1024, 50304], P('dp', ('yax', 'xax'))
- output 4: float32 [1024], P('dp')
All inputs are finite; a program needn't handle non-finite values.
Results may differ from a plain program's by a relative error of at most 0.00831753.
Values are sent between devices in bfloat16 or wider.
A program may use at most 768 MiB of HBM per device.

v0:
```python
import functools

import jax
import jax.numpy as jnp
import numpy as np
from jax import lax
from jax.experimental import pallas as pl
from jax.experimental.pallas import tpu as pltpu
from jax.sharding import PartitionSpec as P

EPS = 1e-6
ROPE_BASE = 10000.0
F32 = jnp.float32
BF16 = jnp.bfloat16
NT = (((1,), (1,)), ((), ()))
EMBED_CHUNKS = 16
EMBED_FIRST = 14


def layer_norm(values_in, gain):
    mean = jnp.mean(values_in, axis=-1, keepdims=True)
    centred = values_in - mean
    var = jnp.mean(centred * centred, axis=-1, keepdims=True)
    return centred * lax.rsqrt(var + EPS) * gain


def row_chunks(total, count):
    cuts = [16 * (total // 16 * i // count) for i in range(count)] + [total]
    return [(cuts[i], cuts[i + 1] - cuts[i]) for i in range(count)]


def kernel(cfg, lens_hbm, hidden, k_hbm, v_hbm, g_attn, g_final, wq_hbm, w_key, w_value, w_gate, w_up,
           w_out, w_down, embed, freq_hbm,
           k_out, v_out, logits_out, norm_out,
           k_buf, v_buf, h_buf, ga_buf, gf_buf, wqt, wq_buf, gu_buf, down_buf, out_buf, kv_buf,
           n_all, q_scr, qx_buf, q2d, snew, krep, vrep, s_scr, od_scr, o_scr, ox_buf, act_scr, act, part_scr,
           pre_buf, rs_scr, rs_buf, f_buf, e_buf, z_scr, st_scr, k_scr, v_scr, norm_scr, s_buf,
           lens, w_query, freq,
           kv_sem, e_own_sem, z_sem, x_send, x_recv, g_send, g_recv, g_last, y_send, y_recv, e_send, e_recv,
           n_recv, n_last, n_send, pre_sem, rs_sem, fxa, fyb, fya, fxb, f_sem, s_sem):
    ys, xs, own, vocab, shift = cfg
    y = lax.axis_index("yax")
    x = lax.axis_index("xax")
    core = lax.rem(x, 2)
    partner = x + 1 - 2 * core
    blk = hidden.shape[1]
    quarter = xs * own
    head_dim = k_hbm.shape[1]
    half = head_dim // 2
    seqs = k_hbm.shape[0]
    slots = k_hbm.shape[2]
    heads = w_query.shape[1] * ys // head_dim
    groups = k_buf.shape[0]
    per = seqs // groups
    window = e_buf.shape[0]

    def lanes(i):
        return pl.ds(pl.multiple_of(i * blk, 128), blk)

    def rows(i, n):
        return pl.ds(pl.multiple_of(i * n, n), n)

    barrier = pltpu.get_barrier_semaphore()

    def signal_row(d, carry):
        pl.semaphore_signal(barrier, inc=1, device_id={"xax": lax.rem(x + d, xs)},
                            device_id_type=pl.DeviceIdType.MESH)
        return carry
    lax.fori_loop(1, xs, signal_row, 0)

    def signal_column(d, carry):
        pl.semaphore_signal(barrier, inc=1, device_id={"yax": lax.rem(y + d, ys)},
                            device_id_type=pl.DeviceIdType.MESH)
        return carry
    lax.fori_loop(1, ys, signal_column, 0)
    small_ins = [pltpu.make_async_copy(a, b, z_sem.at[i])
                 for i, (a, b) in enumerate(((wq_hbm, w_query), (freq_hbm, freq), (lens_hbm, lens)))]
    for copy in small_ins:
        copy.start()
    def cache_copy(g, src, dst, s):
        return pltpu.make_async_copy(src.at[pl.ds(g * per, per)], dst.at[g], kv_sem.at[s, g])

    def start_cache(g, carry):
        cache_copy(g, k_hbm, k_buf, 0).start()
        return carry
    lax.fori_loop(0, groups, start_cache, 0)

    for copy in small_ins:
        copy.wait()
    wqt[...] = w_query[...].astype(F32).T.astype(BF16)

    pl.semaphore_wait(barrier, xs + ys - 2)

    def far(k, n):
        return n // 2 + k // 2 * (2 * lax.rem(k, 2) - 1)

    def arrived(ref, sem):
        pltpu.make_async_copy(ref, ref, sem).wait()

    cols = wqt.shape[0] // xs
    ff = w_gate.shape[1] // xs
    most = pl.ds(0, (xs - 1) * blk)
    x_kinds = {
        "wq": (lambda p: wqt.at[rows(p, cols), :], lambda s: wq_buf.at[y, :, lanes(s)],
               wq_buf.at[y], wq_buf.at[y, :, most]),
        "wo": (lambda p: w_out.at[rows(p, cols), :], lambda s: out_buf.at[y, :, lanes(s)],
               out_buf.at[y], out_buf.at[y, :, most]),
        "down": (lambda p: w_down.at[rows(p, ff), :], lambda s: down_buf.at[y, :, lanes(s)],
                 down_buf.at[y], down_buf.at[y, :, most]),
        "gate": (lambda p: w_gate.at[:, lanes(p)], lambda s: gu_buf.at[rows(s, blk), pl.ds(0, ff)],
                 gu_buf.at[:, pl.ds(0, ff)], gu_buf.at[most, pl.ds(0, ff)]),
        "up": (lambda p: w_up.at[:, lanes(p)], lambda s: gu_buf.at[rows(s, blk), pl.ds(ff, ff)],
               gu_buf.at[:, pl.ds(ff, ff)], gu_buf.at[most, pl.ds(ff, ff)]),
        "q": (lambda p: q_scr.at[rows(p, own), :], lambda s: qx_buf.at[s],
              qx_buf, qx_buf.at[pl.ds(0, xs - 1)]),
        "o": (lambda p: o_scr.at[p], lambda s: ox_buf.at[rows(s, own), :],
              ox_buf, ox_buf.at[pl.ds(0, (xs - 1) * own), :]),
    }
    x_index = {name: i for i, name in enumerate(x_kinds)}

    def x_start(name):
        src, dst = x_kinds[name][:2]
        k = x_index[name]

        def body(k1, carry):
            p = lax.rem(x + far(k1, xs), xs)
            pltpu.make_async_remote_copy(
                src_ref=src(p), dst_ref=dst(x), send_sem=x_send.at[k], recv_sem=x_recv.at[k],
                device_id={"xax": p}, device_id_type=pl.DeviceIdType.MESH).start()
            return carry
        lax.fori_loop(1, xs, body, 0)
        pltpu.make_async_copy(src(x), dst(x), x_recv.at[k]).start()

    def x_wait(name):
        arrived(x_kinds[name][2], x_recv.at[x_index[name]])

    def x_drain(name):
        arrived(x_kinds[name][3], x_send.at[x_index[name]])

    chips = xs // 2
    g_kinds = {
        "hidden": (hidden.at[rows(y, quarter), :], lambda s: h_buf.at[:, lanes(s)], h_buf),
        "ga": (g_attn, lambda s: ga_buf.at[:, lanes(s)], ga_buf),
        "gf": (g_final, lambda s: gf_buf.at[:, lanes(s)], gf_buf),
        "wk": (w_key, lambda s: kv_buf.at[pl.ds(0, head_dim), lanes(s)], kv_buf.at[pl.ds(0, head_dim), :]),
        "wv": (w_value, lambda s: kv_buf.at[pl.ds(head_dim, head_dim), lanes(s)],
               kv_buf.at[pl.ds(head_dim, head_dim), :]),
    }
    g_index = {name: i for i, name in enumerate(g_kinds)}

    def g_copy(name, i, sender):
        src, dst, _ = g_kinds[name]
        k = g_index[name]
        return pltpu.make_async_remote_copy(
            src_ref=src, dst_ref=dst(sender), send_sem=g_send.at[k], recv_sem=g_recv.at[k, i],
            device_id={"xax": lax.rem(x + 2 * i, xs)}, device_id_type=pl.DeviceIdType.MESH)

    def g_pass(name, sender, source):
        k = g_index[name]
        return pltpu.make_async_remote_copy(
            src_ref=source, dst_ref=g_kinds[name][1](sender), send_sem=g_send.at[k], recv_sem=g_last.at[k],
            device_id={"xax": partner}, device_id_type=pl.DeviceIdType.MESH)

    def g_start(name):
        def body(i, carry):
            g_copy(name, far(i, chips), x).start()
            return carry
        lax.fori_loop(1, chips, body, 0)
        src, dst, _ = g_kinds[name]
        g_pass(name, x, src).start()
        pltpu.make_async_copy(src, dst(x), g_last.at[g_index[name]]).start()

    def g_forward(name):
        def body(i, carry):
            sender = lax.rem(x + xs - 2 * i, xs)
            g_copy(name, i, sender).wait_recv()
            g_pass(name, sender, g_kinds[name][1](sender)).start()
            return carry
        lax.fori_loop(1, chips, body, 0)

    def g_wait(name):
        whole = g_kinds[name][2]
        arrived(whole.at[:, pl.ds(0, (chips + 1) * blk)], g_last.at[g_index[name]])

    def g_drain(name):
        arrived(g_kinds[name][2].at[:, most], g_send.at[g_index[name]])

    y_kinds = {"wq": wq_buf, "wo": out_buf, "down": down_buf}
    y_index = {name: i for i, name in enumerate(y_kinds)}
    others = pl.ds(0, ys - 1)

    def y_start(name):
        buf = y_kinds[name]
        k = y_index[name]

        def body(d, carry):
            pltpu.make_async_remote_copy(
                src_ref=buf.at[y], dst_ref=buf.at[y], send_sem=y_send.at[k], recv_sem=y_recv.at[k],
                device_id={"yax": lax.rem(y + far(d, ys), ys)}, device_id_type=pl.DeviceIdType.MESH).start()
            return carry
        lax.fori_loop(1, ys, body, 0)

    def y_wait(name):
        arrived(y_kinds[name].at[others], y_recv.at[y_index[name]])

    def y_drain(name):
        arrived(y_kinds[name].at[others], y_send.at[y_index[name]])

    e_parts = row_chunks(window, EMBED_CHUNKS)

    def e_first(p):
        return p * vocab - lax.rem(p, 2) * shift

    def e_own():
        return pltpu.make_async_copy(
            embed.at[pl.ds(pl.multiple_of(e_first(x), 8), window), :], e_buf.at[:, lanes(x)], e_own_sem)

    def e_start(c):
        r0, n = e_parts[c]

        def body(d, carry):
            p = lax.rem(x + d, xs)
            pltpu.make_async_remote_copy(
                src_ref=embed.at[pl.ds(pl.multiple_of(e_first(p) + r0, 8), n), :],
                dst_ref=e_buf.at[pl.ds(r0, n), lanes(x)], send_sem=e_send,
                recv_sem=e_recv.at[int(c >= EMBED_FIRST)],
                device_id={"xax": p}, device_id_type=pl.DeviceIdType.MESH).start()
            return carry
        lax.fori_loop(1, xs, body, 0)

    x_start("wq")
    for name in ("hidden", "ga"):
        g_start(name)
    for name in ("wo", "down"):
        x_start(name)
    for name in ("wk", "wv", "gf"):
        g_start(name)
    e_start(0)
    e_own().start()

    def start_cache_v(g, carry):
        cache_copy(g, v_hbm, v_buf, 1).start()
        return carry
    lax.fori_loop(0, groups, start_cache_v, 0)

    x_wait("wq")
    y_start("wq")
    for name in ("hidden", "ga"):
        g_forward(name)
    for name in ("hidden", "ga"):
        g_wait(name)
    my_rows = rows(y, quarter)
    n_all[my_rows, :] = layer_norm(h_buf[...].astype(F32), ga_buf[...]).astype(BF16)

    part = quarter // 2

    def n_rows(j, c):
        return pl.ds(pl.multiple_of(j * quarter + c * part, part), part)

    def n_copy(d, sender):
        r = n_rows(sender, core)
        return pltpu.make_async_remote_copy(
            src_ref=n_all.at[r, :], dst_ref=n_all.at[r, :], send_sem=n_send.at[0],
            recv_sem=n_recv.at[d], device_id={"yax": lax.rem(y + d, ys)},
            device_id_type=pl.DeviceIdType.MESH)

    def n_pass(d, c):
        r = n_rows(lax.rem(y + ys - d, ys), c)
        return pltpu.make_async_remote_copy(
            src_ref=n_all.at[r, :], dst_ref=n_all.at[r, :], send_sem=n_send.at[1],
            recv_sem=n_last.at[d], device_id={"xax": partner},
            device_id_type=pl.DeviceIdType.MESH)

    x_wait("wo")
    y_start("wo")
    y_wait("wq")
    wq_all = wq_buf[...].reshape(ys * cols, xs * blk)
    q_scr[...] = lax.dot_general(n_all[my_rows, :], wq_all, NT, preferred_element_type=F32).astype(BF16)
    x_start("q")
    x_start("gate")
    x_start("up")

    def n_start(d, carry):
        n_copy(far(d, ys), y).start()
        return carry
    lax.fori_loop(1, ys, n_start, 0)
    x_wait("down")
    y_start("down")
    for c in range(1, 7):
        e_start(c)

    row_id = lax.broadcasted_iota(jnp.int32, (own, 4 * half), 0)
    first_row = (y * xs + x) * own
    position = jnp.zeros((own, 4 * half), jnp.int32)
    for b in range(own):
        position = jnp.where(row_id == b, lens[first_row + b], position)
    angle = position.astype(F32) * freq[...]
    cos_a = jnp.cos(angle)
    sin_a = jnp.sin(angle)
    for name in ("wk", "wv", "gf"):
        g_forward(name)
    for name in ("wk", "wv", "gf"):
        g_wait(name)
    mine = y * xs + x
    n_own = n_all[rows(mine, own), :]
    kv = lax.dot_general(n_own, kv_buf[...], NT, preferred_element_type=F32).astype(BF16).astype(F32)
    k1 = kv[:, :half]
    k2 = kv[:, half:head_dim]
    c1 = cos_a[:, :half]
    s1 = sin_a[:, :half]
    key = jnp.concatenate([k1 * c1 - k2 * s1, k2 * c1 + k1 * s1], axis=1).astype(BF16)
    value = kv[:, head_dim:].astype(BF16)
    k_scr[...] = key
    v_scr[...] = value
    small_outs = [pltpu.make_async_copy(k_scr, k_out, z_sem.at[0]),
                  pltpu.make_async_copy(v_scr, v_out, z_sem.at[1])]
    for copy in small_outs:
        copy.start()
    for h in range(heads):
        krep[pl.ds(h, own, stride=heads), :] = key.astype(F32)
        vrep[pl.ds(h, own, stride=heads), :] = value.astype(F32)

    x_wait("q")
    for xc in range(xs // 2):
        qa = qx_buf[2 * xc].astype(F32)
        qb = qx_buf[2 * xc + 1].astype(F32)
        ra = (qa * cos_a - qb * sin_a).astype(BF16).astype(F32)
        rb = (qb * cos_a + qa * sin_a).astype(BF16).astype(F32)
        for yc in range(ys):
            pair = jnp.concatenate([ra[:, yc * half:(yc + 1) * half], rb[:, yc * half:(yc + 1) * half]], axis=1)
            q2d[pl.ds(xc * ys + yc, own, stride=heads), :] = pair
    scale = head_dim ** -0.5
    snew[...] = jnp.sum(q2d[...] * krep[...], axis=1, keepdims=True) * scale

    gr = per * heads
    seg_r = lax.broadcasted_iota(jnp.int32, (gr, per * head_dim), 0) // heads
    seg_c = lax.broadcasted_iota(jnp.int32, (gr, per * head_dim), 1) // head_dim
    diag = (seg_r == seg_c).astype(F32)
    tile = min(512, slots)
    row_g = lax.broadcasted_iota(jnp.int32, (gr, 1), 0) // heads
    lane_g = lax.broadcasted_iota(jnp.int32, (gr, tile), 1)

    def attend(g, carry):
        cache_copy(g, k_hbm, k_buf, 0).wait()
        qg = q2d[rows(g, gr), :]
        qbd = (jnp.concatenate([qg] * per, axis=1) * diag).astype(BF16)
        len_g = jnp.zeros((gr, 1), jnp.int32)
        for s in range(per):
            len_g = jnp.where(row_g == s, lens[first_row + g * per + s], len_g)
        new = snew[rows(g, gr), :]
        top = jnp.full((gr, tile), -jnp.inf, F32)
        kg = k_buf.at[g]
        vg = v_buf.at[g]
        for c in range(slots // tile):
            kc = kg[:, :, pl.ds(c * tile, tile)].reshape(per * head_dim, tile)
            sc = jnp.dot(qbd, kc, preferred_element_type=F32) * scale
            sc = jnp.where(lane_g < len_g - c * tile, sc, -jnp.inf)
            s_scr[:, pl.ds(c * tile, tile)] = sc
            top = jnp.maximum(top, sc)
        row_max = jnp.maximum(jnp.max(top, axis=1, keepdims=True), new)
        total = jnp.zeros((gr, tile), F32)
        for c in range(slots // tile):
            ex = jnp.exp(s_scr[:, pl.ds(c * tile, tile)] - row_max)
            s_scr[:, pl.ds(c * tile, tile)] = ex
            total = total + ex
        w_new = jnp.exp(new - row_max)
        den = jnp.sum(total, axis=1, keepdims=True) + w_new
        inv = 1.0 / den
        cache_copy(g, v_hbm, v_buf, 1).wait()
        mixed = jnp.zeros((gr, per * head_dim), F32)
        for c in range(slots // tile):
            pr = (s_scr[:, pl.ds(c * tile, tile)] * inv).astype(BF16)
            vc = vg[:, :, pl.ds(c * tile, tile)].reshape(per * head_dim, tile)
            mixed = mixed + lax.dot_general(pr, vc, NT, preferred_element_type=F32)
        add = (w_new * inv).astype(BF16).astype(F32) * vrep[rows(g, gr), :]
        for s in range(per):
            od_scr[pl.ds(pl.multiple_of(g * gr + s * heads, heads), heads), :] = (
                mixed[s * heads:(s + 1) * heads, s * head_dim:(s + 1) * head_dim]
                + add[s * heads:(s + 1) * heads, :])
        return carry

    lax.fori_loop(0, groups, attend, 0)
    for xc in range(xs // 2):
        parts = [od_scr[pl.ds(xc * ys + yc, own, stride=heads), :] for yc in range(ys)]
        o_scr[2 * xc] = jnp.concatenate([p[:, :half] for p in parts], axis=1).astype(BF16)
        o_scr[2 * xc + 1] = jnp.concatenate([p[:, half:] for p in parts], axis=1).astype(BF16)
    x_start("o")
    for c in range(7, 12):
        e_start(c)

    def act_copy(dest):
        return pltpu.make_async_remote_copy(
            src_ref=act_scr.at[dest], dst_ref=act.at[:, pl.ds(pl.multiple_of(y * ff, ff), ff)],
            send_sem=y_send.at[len(y_kinds)], recv_sem=y_recv.at[len(y_kinds)],
            device_id={"yax": dest}, device_id_type=pl.DeviceIdType.MESH)

    x_wait("gate")
    x_wait("up")

    def feed(d, carry):
        @pl.when(d < ys - 1)
        def _():
            n_copy(d + 1, lax.rem(y + ys - d - 1, ys)).wait_recv()
            n_pass(d + 1, core).start()
        j = lax.rem(y + ys - d, ys)

        @pl.when(d > 0)
        def _():
            n_pass(d, 1 - core).wait_recv()
        gu = jnp.dot(n_all[rows(j, quarter), :], gu_buf[...], preferred_element_type=F32)
        gu = gu.astype(BF16).astype(F32)
        gate = gu[:, :ff]
        act_scr[j] = (gate * jax.nn.sigmoid(gate) * gu[:, ff:]).astype(BF16)

        @pl.when(d > 0)
        def _():
            act_copy(j).start()
        return carry
    lax.fori_loop(0, ys, feed, 0)
    act[:, pl.ds(pl.multiple_of(y * ff, ff), ff)] = act_scr[y]
    y_wait("wo")
    x_wait("o")
    part_scr[...] = jnp.dot(
        ox_buf[...], out_buf[...].reshape(ys * cols, xs * blk), preferred_element_type=F32)
    y_wait("down")

    arrived(act_scr.at[others], y_recv.at[len(y_kinds)])

    down_all = down_buf[...].reshape(ys * ff, xs * blk)
    part_scr[...] = part_scr[...] + jnp.dot(act[...], down_all, preferred_element_type=F32)

    def branch(c):
        for i in range(chips):
            rs_scr[c, i] = part_scr[pl.ds(pl.multiple_of((2 * i + c) * own, own), own), :]

    def pre_copy():
        return pltpu.make_async_remote_copy(
            src_ref=rs_scr.at[1 - core], dst_ref=pre_buf, send_sem=pre_sem.at[0], recv_sem=pre_sem.at[1],
            device_id={"xax": partner}, device_id_type=pl.DeviceIdType.MESH)

    def rs_copy(dest):
        return pltpu.make_async_remote_copy(
            src_ref=rs_scr.at[core, dest], dst_ref=rs_buf.at[chip], send_sem=rs_sem.at[0],
            recv_sem=rs_sem.at[1], device_id={"xax": 2 * dest + core},
            device_id_type=pl.DeviceIdType.MESH)

    chip = x // 2
    branch(1 - core)
    pre_copy().start()
    branch(core)
    pre_copy().wait_recv()
    rs_scr[core] = rs_scr[core] + pre_buf[...]

    def rs_start(i, carry):
        rs_copy(lax.rem(chip + far(i, chips), chips)).start()
        return carry
    lax.fori_loop(1, chips, rs_start, 0)
    e_start(12)
    arrived(rs_buf.at[pl.ds(0, chips - 1)], rs_sem.at[1])
    rs_buf[chip] = rs_scr[core, chip]
    res = h_buf[rows(x, own), :].astype(F32) + jnp.sum(rs_buf[...], axis=0)
    f_buf[rows(mine, own), :] = layer_norm(res, gf_buf[...]).astype(BF16)

    piece = own // 2

    def f_half(sy, sx, h):
        return f_buf.at[pl.ds(pl.multiple_of((sy * xs + sx) * own + h * piece, piece), piece), :]

    def f_over_x(i, h, sy, sx, sem):
        return pltpu.make_async_remote_copy(
            src_ref=f_half(sy, sx, h), dst_ref=f_half(sy, sx, h), send_sem=f_sem.at[0], recv_sem=sem,
            device_id={"xax": lax.rem(x + 2 * i, xs)}, device_id_type=pl.DeviceIdType.MESH)

    def f_over_y(d, h, sy, sx, sem):
        return pltpu.make_async_remote_copy(
            src_ref=f_half(sy, sx, h), dst_ref=f_half(sy, sx, h), send_sem=f_sem.at[0], recv_sem=sem,
            device_id={"yax": lax.rem(y + d, ys)}, device_id_type=pl.DeviceIdType.MESH)

    def f_pass(d, h, sy, sx):
        pltpu.make_async_remote_copy(
            src_ref=f_half(sy, sx, h), dst_ref=f_half(sy, sx, h), send_sem=f_sem.at[1],
            recv_sem=f_sem.at[2 + d], device_id={"xax": partner},
            device_id_type=pl.DeviceIdType.MESH).start()

    def from_y(d):
        return lax.rem(y + ys - d, ys)

    def from_x(i):
        return lax.rem(x + xs - 2 * i, xs)

    def spread_y(i):
        def body(d, carry):
            f_over_y(far(d, ys), 0, y, from_x(i), fya.at[far(d, ys), i]).start()
            return carry
        lax.fori_loop(1, ys, body, 0)

    def spread_x(d):
        def body(i, carry):
            f_over_x(far(i, chips), 1, from_y(d), x, fxb.at[d, far(i, chips)]).start()
            return carry
        lax.fori_loop(1, chips, body, 0)

    def first_x(i, carry):
        f_over_x(far(i, chips), 0, y, x, fxa.at[far(i, chips)]).start()
        return carry
    lax.fori_loop(1, chips, first_x, 0)

    def first_y(d, carry):
        f_over_y(far(d, ys), 1, y, x, fyb.at[far(d, ys)]).start()
        return carry
    lax.fori_loop(1, ys, first_y, 0)
    spread_y(0)
    spread_x(0)
    f_pass(0, 0, y, x)
    f_pass(0, 1, y, x)
    e_start(13)
    for i in sorted(range(1, max(chips, ys)), key=lambda d: (min(d, max(chips, ys) - d), d)):
        if i < chips:
            f_over_x(i, 0, y, from_x(i), fxa.at[i]).wait_recv()
            spread_y(i)
            f_pass(0, 0, y, from_x(i))
        if i < ys:
            f_over_y(i, 1, from_y(i), x, fyb.at[i]).wait_recv()
            spread_x(i)
            f_pass(i, 1, from_y(i), x)
    for c in range(14, EMBED_CHUNKS):
        e_start(c)

    def collect(d):
        def body(i, carry):
            @pl.when(d > 0)
            def _():
                f_over_y(d, 0, from_y(d), from_x(i), fya.at[d, i]).wait_recv()
                f_pass(d, 0, from_y(d), from_x(i))

            @pl.when(i > 0)
            def _():
                f_over_x(i, 1, from_y(d), from_x(i), fxb.at[d, i]).wait_recv()
                f_pass(d, 1, from_y(d), from_x(i))
            return carry
        lax.fori_loop(0, chips, body, 0)

    for name in x_kinds:
        x_drain(name)
    for name in g_kinds:
        g_drain(name)
    for name in y_kinds:
        y_drain(name)
    arrived(act_scr.at[others], y_send.at[len(y_kinds)])
    for i in range(2):
        arrived(n_all.at[pl.ds(0, (ys - 1) * part), :], n_send.at[i])
    pre_copy().wait_send()
    arrived(rs_buf.at[pl.ds(0, chips - 1)], rs_sem.at[0])
    for copy in small_outs:
        copy.wait()

    cut = e_parts[EMBED_FIRST][0]
    skip = core * shift
    half_block = pl.ds(0, chips * own)

    def nearest(k):
        return k + k // 2 * (1 - 2 * lax.rem(k, 2))

    def z_copy(j, r0, n):
        return pltpu.make_async_copy(
            z_scr.at[j, pl.ds(r0, n), :], logits_out.at[pl.ds(r0, n), rows(j, quarter)], z_sem.at[2])

    def block(j, r0, n, pieces):
        r = pl.ds(r0, n)
        z_scr[j, r, :] = lax.dot_general(e_buf[r, :], f_buf[rows(j, quarter), :], NT, preferred_element_type=F32)
        z_copy(j, r0, n).start()
        stats = []
        for q0, m in row_chunks(n, pieces):
            z = z_scr[j, pl.ds(r0 + q0, m), :]
            if shift and (r0 + q0 == 0 or r0 + q0 + m == window):
                index = lax.broadcasted_iota(jnp.int32, z.shape, 0) + (r0 + q0)
                z = jnp.where(jnp.logical_and(index >= skip, index < skip + vocab), z, -jnp.inf)
            top = jnp.max(z, axis=0, keepdims=True)
            stats.append((top, jnp.sum(jnp.exp(z - top), axis=0, keepdims=True)))
        return stats

    def put(j, stats):
        top = functools.reduce(jnp.maximum, [t for t, _ in stats])
        st_scr[0:1, rows(j, quarter)] = top
        st_scr[1:2, rows(j, quarter)] = sum(t * jnp.exp(m - top) for m, t in stats)

    def head(k, carry):
        d = nearest(k)
        j = from_y(d)
        arrived(f_buf.at[half_block, :], f_sem.at[2 + d])
        put(j, block(j, 0, cut, 4))

        @pl.when(k < ys - 2)
        def _():
            collect(nearest(k + 2))
        return carry

    def head_rest(j, carry):
        before = (st_scr[0:1, rows(j, quarter)], st_scr[1:2, rows(j, quarter)])
        put(j, [before] + block(j, cut, window - cut, 1))
        return carry

    for k in range(min(2, ys)):
        collect(nearest(k))
    e_own().wait()
    arrived(e_buf.at[pl.ds(0, cut), most], e_recv.at[0])

    lax.fori_loop(0, ys, head, 0)
    arrived(e_buf.at[pl.ds(cut, window - cut), most], e_recv.at[1])
    lax.fori_loop(0, ys, head_rest, 0)

    for k in range(ys):
        dy = (ys // 2 + k) % ys
        for dx in range(xs):
            if dy + dx > 0:
                pltpu.make_async_remote_copy(
                    src_ref=st_scr, dst_ref=s_buf.at[mine], send_sem=s_sem.at[0], recv_sem=s_sem.at[1],
                    device_id={"yax": lax.rem(y + dy, ys), "xax": lax.rem(x + dx, xs)},
                    device_id_type=pl.DeviceIdType.MESH).start()
    s_buf[mine] = st_scr[...]

    arrived(e_buf.at[:, most], e_send)
    arrived(f_buf.at[pl.ds(0, 2 * (ys * chips - 1) * piece), :], f_sem.at[0])
    arrived(f_buf.at[pl.ds(0, ys * chips * own), :], f_sem.at[1])
    arrived(z_scr, z_sem.at[2])
    everyone = s_buf.at[pl.ds(0, ys * xs - 1)]
    arrived(everyone, s_sem.at[1])
    tops = s_buf[:, 0, :]
    best = jnp.max(tops, axis=0, keepdims=True)
    whole = jnp.sum(s_buf[:, 1, :] * jnp.exp(tops - best), axis=0, keepdims=True)
    norm_scr[...] = best + jnp.log(whole)
    norm_copy = pltpu.make_async_copy(norm_scr, norm_out, z_sem.at[0])
    norm_copy.start()
    arrived(everyone, s_sem.at[0])
    norm_copy.wait()


def finish_kernel(shift, z_hbm, norm_hbm, key, value, out_hbm, k_out, v_out, norm_out,
                  z_buf, o_buf, norm, k_scr, v_scr, in_sem, out_sem):
    count, n, width = o_buf.shape

    def load(i):
        return pltpu.make_async_copy(z_hbm.at[:, pl.ds(i * width, width)], z_buf.at[i], in_sem.at[i])

    def save(i):
        return pltpu.make_async_copy(o_buf.at[i], out_hbm.at[:, pl.ds(i * width, width)], out_sem.at[i])

    small = ((norm_hbm, norm, norm_out), (key, k_scr, k_out), (value, v_scr, v_out))
    small_in = [pltpu.make_async_copy(a, b, in_sem.at[count + i]) for i, (a, b, _) in enumerate(small)]
    small_out = [pltpu.make_async_copy(b, c, out_sem.at[count + i]) for i, (_, b, c) in enumerate(small)]
    small_in[0].start()
    for i in range(count):
        load(i).start()
    for copy in small_in[1:]:
        copy.start()
    small_in[0].wait()
    small_out[0].start()
    odd = lax.rem(lax.axis_index("xax"), 2) == 1
    for i in range(count):
        row = norm[:, pl.ds(i * width, width)]
        load(i).wait()
        if shift:
            @pl.when(odd)
            def _():
                o_buf[i] = z_buf[i, pl.ds(shift, n), :] - row

            @pl.when(jnp.logical_not(odd))
            def _():
                o_buf[i] = z_buf[i, pl.ds(0, n), :] - row
        else:
            o_buf[i] = z_buf[i] - row
        save(i).start()
    for i in (1, 2):
        small_in[i].wait()
        small_out[i].start()
    for copy in small_out:
        copy.wait()
    for i in range(count):
        save(i).wait()


def solution(mesh):
    ys = mesh.shape["yax"]
    xs = mesh.shape["xax"]
    row_spec = P(("dp", "yax", "xax"))

    def local_step(hidden, cache_len, k_cache, v_cache, g_attn, w_query, w_key, w_value,
                   w_gate, w_up, w_out, w_down, g_final, embedding):
        batch, blk = hidden.shape
        own, slots, head_dim = k_cache.shape
        width = blk * xs
        vocab = embedding.shape[0] // xs
        shift = vocab % 8
        window = -(-vocab // 8) * 8
        half = head_dim // 2
        quarter = xs * own
        cols = w_query.shape[1] // xs
        ff = w_gate.shape[1] // xs
        heads = w_query.shape[1] * ys // head_dim
        per = 4
        groups = own // per
        freq_row = (ROPE_BASE ** (-(np.arange(half, dtype=np.float32) * 2.0) / head_dim)).astype(np.float32)
        freq = jnp.asarray(np.tile(freq_row, 4)[None, :])
        any_spec = pl.BlockSpec(memory_space=pl.ANY)
        dma = pltpu.SemaphoreType.DMA
        chips = xs // 2
        scratch = [
            pltpu.VMEM((groups, per, head_dim, slots), BF16),
            pltpu.VMEM((groups, per, head_dim, slots), BF16),
            pltpu.VMEM((quarter, width), BF16),
            pltpu.VMEM((1, width), F32),
            pltpu.VMEM((1, width), F32),
            pltpu.VMEM((w_query.shape[1], blk), BF16),
            pltpu.VMEM((ys, cols, width), BF16),
            pltpu.VMEM((width, 2 * ff), BF16),
            pltpu.VMEM((ys, ff, width), BF16),
            pltpu.VMEM((ys, cols, width), BF16),
            pltpu.VMEM((2 * head_dim, width), BF16),
            pltpu.VMEM((batch, width), BF16),
            pltpu.VMEM((quarter, ys * cols), BF16),
            pltpu.VMEM((xs, own, ys * cols), BF16),
            pltpu.VMEM((own * heads, head_dim), F32),
            pltpu.VMEM((own * heads, 1), F32),
            pltpu.VMEM((own * heads, head_dim), F32),
            pltpu.VMEM((own * heads, head_dim), F32),
            pltpu.VMEM((per * heads, slots), F32),
            pltpu.VMEM((own * heads, head_dim), F32),
            pltpu.VMEM((xs, own, ys * cols), BF16),
            pltpu.VMEM((quarter, ys * cols), BF16),
            pltpu.VMEM((ys, quarter, ff), BF16),
            pltpu.VMEM((quarter, ys * ff), BF16),
            pltpu.VMEM((quarter, width), F32),
            pltpu.VMEM((chips, own, width), F32),
            pltpu.VMEM((2, chips, own, width), F32),
            pltpu.VMEM((chips, own, width), F32),
            pltpu.VMEM((batch, width), BF16),
            pltpu.VMEM((window, width), BF16),
            pltpu.VMEM((ys, window, quarter), F32),
            pltpu.VMEM((2, batch), F32),
            pltpu.VMEM((own, head_dim), BF16),
            pltpu.VMEM((own, head_dim), BF16),
            pltpu.VMEM((1, batch), F32),
            pltpu.VMEM((ys * xs, 2, batch), F32),
            pltpu.SMEM(cache_len.shape, jnp.int32),
            pltpu.VMEM(w_query.shape, BF16),
            pltpu.VMEM((1, 4 * half), F32),
            dma((2, groups)), dma, dma((3,)), dma((7,)), dma((7,)),
            dma((5,)), dma((5, chips)), dma((5,)), dma((4,)), dma((4,)), dma, dma((2,)),
            dma((ys,)), dma((ys,)), dma((2,)), dma((2,)), dma((2,)),
            dma((chips,)), dma((ys,)), dma((ys, chips)), dma((ys, chips)), dma((2 + ys,)), dma((2,)),
        ]
        cfg = (ys, xs, own, vocab, shift)
        key_new, value_new, logits, norm = pl.pallas_call(
            functools.partial(kernel, cfg),
            name="decode_layer",
            out_shape=(
                jax.ShapeDtypeStruct((own, head_dim), BF16),
                jax.ShapeDtypeStruct((own, head_dim), BF16),
                jax.ShapeDtypeStruct((window, batch), F32),
                jax.ShapeDtypeStruct((1, batch), F32)),
            in_specs=[any_spec] * 15,
            out_specs=(any_spec, any_spec, any_spec, any_spec),
            scratch_shapes=scratch,
            compiler_params=pltpu.CompilerParams(
                collective_id=0, has_side_effects=True, vmem_limit_bytes=67043328),
        )(cache_len, hidden, k_cache.transpose(0, 2, 1), v_cache.transpose(0, 2, 1),
          g_attn[None, :], g_final[None, :], w_query, w_key.T, w_value.T, w_gate, w_up, w_out, w_down,
          embedding, freq)
        count = 8
        log_probs, key_new, value_new, norm = pl.pallas_call(
            functools.partial(finish_kernel, shift),
            name="finish",
            out_shape=(
                jax.ShapeDtypeStruct((vocab, batch), F32),
                jax.ShapeDtypeStruct((own, head_dim), BF16),
                jax.ShapeDtypeStruct((own, head_dim), BF16),
                jax.ShapeDtypeStruct((1, batch), F32)),
            in_specs=[any_spec] * 4,
            out_specs=(any_spec,) * 4,
            scratch_shapes=[
                pltpu.VMEM((count, window, batch // count), F32),
                pltpu.VMEM((count, vocab, batch // count), F32),
                pltpu.VMEM((1, batch), F32), pltpu.VMEM((own, head_dim), BF16), pltpu.VMEM((own, head_dim), BF16),
                dma((count + 3,)), dma((count + 3,))],
        )(logits, norm, key_new, value_new)
        return key_new, value_new, log_probs.T, norm[0]

    in_specs = (P("dp", "xax"), P("dp"), row_spec, row_spec, P("xax"), P("xax", "yax"),
                P("xax", None), P("xax", None), P("xax", "yax"), P("xax", "yax"),
                P("yax", "xax"), P("yax", "xax"), P("xax"), P("yax", "xax"))
    out_specs = (row_spec, row_spec, P("dp", ("yax", "xax")), P("dp"))
    return jax.shard_map(local_step, mesh=mesh, in_specs=in_specs, out_specs=out_specs, check_vma=False)
```

profile of v0, /device:TPU:97, one launch (start us, length us, event | category | flops | bytes accessed | tf_op | source)
XLA Modules:
  0.0 89.9 jit_solution(5126059559088273909)
XLA Ops:
  0.6 83.4 %decode_layer.1 = (bf16[32,64]{1,0:T(8,128)(2,1)}, bf16[32,64]{1,0:T(8,128)(2,1)}, f32[1576,1024]{1,0:T(8,128)}, f32[1,1024]{1,0:T(1,128)}) custom-call(s32[1024]{0:T(1024)} %lens_hbm.1, bf16[1024,128]{1,0:T(8,128)(2,1)} %hidden.1, bf16[32,64,4096]{2,1,0:T(8,128)(2,1)} %bitcast.8, bf16[32,64,4096]{2,1,0:T(8,128)(2,1)} %bitcast.9, f32[1,128]{1,0:T(1,128)} %bitcast.12, ...), custom_call_target="tpu_custom_call" | custom-call | tf_op jit(solution)/shard_map/decode_layer/pallas_call | solution.py:753
  84.1 5.8 %finish.1 = (f32[1572,1024]{1,0:T(8,128)}, bf16[32,64]{1,0:T(8,128)(2,1)}, bf16[32,64]{1,0:T(8,128)(2,1)}, f32[1,1024]{1,0:T(1,128)}) custom-call(f32[1576,1024]{1,0:T(8,128)} %get-tuple-element.12.z_hbm, f32[1,1024]{1,0:T(1,128)} %get-tuple-element.13.norm_hbm, bf16[32,64]{1,0:T(8,128)(2,1)} %get-tuple-element.14.key, bf16[32,64]{1,0:T(8,128)(2,1)} %get-tuple-element.15.value), custom_call_target="tpu_custom_call" | custom-call | tf_op jit(solution)/shard_map/finish/pallas_call | solution.py:770
where the time goes:
time: 90 us; the launch traced here: 89.9 us
  Pallas kernels  89.2 us (99%)
    pallas_call x1, Pallas kernels, local_step(): pl.pallas_call(functools.partial(kernel, cfg), name='decode_layer', out_s...  83.4 us
    pallas_call x1, Pallas kernels, local_step(): pl.pallas_call(functools.partial(finish_kernel, shift), name='finish', ou...  5.81 us

commit v1 on v0

--- a/solution.py
+++ b/solution.py
@@ -171,7 +171,8 @@
         pltpu.make_async_copy(src, dst(x), g_last.at[g_index[name]]).start()
 
     def g_forward(name):
-        def body(i, carry):
+        def body(k1, carry):
+            i = k1 + k1 // 2 * (1 - 2 * lax.rem(k1, 2))
             sender = lax.rem(x + xs - 2 * i, xs)
             g_copy(name, i, sender).wait_recv()
             g_pass(name, sender, g_kinds[name][1](sender)).start()

time: 90 us -> 90 us (level)
  no operation moved by 1% of the time
where the time goes in v1:
time: 90 us; the launch traced here: 89.9 us
  Pallas kernels  89.2 us (99%)
    pallas_call x1, Pallas kernels, local_step(): pl.pallas_call(functools.partial(kernel, cfg), name='decode_layer', out_s...  83.4 us
    pallas_call x1, Pallas kernels, local_step(): pl.pallas_call(functools.partial(finish_kernel, shift), name='finish', ou...  5.81 us

profile of v1, /device:TPU:97, one launch (start us, length us, event | category | flops | bytes accessed | tf_op | source)
XLA Modules:
  0.0 89.9 jit_solution(15061204390732475471)
XLA Ops:
  0.6 83.4 %decode_layer.1 = (bf16[32,64]{1,0:T(8,128)(2,1)}, bf16[32,64]{1,0:T(8,128)(2,1)}, f32[1576,1024]{1,0:T(8,128)}, f32[1,1024]{1,0:T(1,128)}) custom-call(s32[1024]{0:T(1024)} %lens_hbm.1, bf16[1024,128]{1,0:T(8,128)(2,1)} %hidden.1, bf16[32,64,4096]{2,1,0:T(8,128)(2,1)} %bitcast.8, bf16[32,64,4096]{2,1,0:T(8,128)(2,1)} %bitcast.9, f32[1,128]{1,0:T(1,128)} %bitcast.12, ...), custom_call_target="tpu_custom_call" | custom-call | tf_op jit(solution)/shard_map/decode_layer/pallas_call | solution.py:754
  84.1 5.8 %finish.1 = (f32[1572,1024]{1,0:T(8,128)}, bf16[32,64]{1,0:T(8,128)(2,1)}, bf16[32,64]{1,0:T(8,128)(2,1)}, f32[1,1024]{1,0:T(1,128)}) custom-call(f32[1576,1024]{1,0:T(8,128)} %get-tuple-element.12.z_hbm, f32[1,1024]{1,0:T(1,128)} %get-tuple-element.13.norm_hbm, bf16[32,64]{1,0:T(8,128)(2,1)} %get-tuple-element.14.key, bf16[32,64]{1,0:T(8,128)(2,1)} %get-tuple-element.15.value), custom_call_target="tpu_custom_call" | custom-call | tf_op jit(solution)/shard_map/finish/pallas_call | solution.py:771
